TPU v7x, 32 devices: a whole 2x2x4 slice. The times are simulated.
32 devices in a mesh: dp: 16 (over z, y, core), tensor: 2 (over x).
Axes of the slice: x: 2, y: 2, z: 4, core: 2. Of those that a mesh axis runs over, the one named last changes fastest.
Arguments:
- activations: bfloat16 [32768, 1024], P(('dp', 'tensor')), may hold values from -6 to 6
- gradients: bfloat16 [32768, 5472], P('dp', 'tensor'), may hold values from -6 to 6
- act_history: float32 [2, 16, 1024], P('tensor'), may hold values from 0.1 to 4
- grad_history: float32 [16, 5472], P(None, 'tensor'), may hold values from 0.1 to 4
- owner_rank: int32 [1024], replicated, may hold values from 0 to 1
- history_slot: int32 [6496], replicated, may hold values from 0 to 15
Outputs:
- weight_grad: float32 [1024, 5472], P('dp', 'tensor')
- act_history_out: float32 [2, 16, 1024], P('tensor')
- grad_history_out: float32 [16, 5472], P(None, 'tensor')
All inputs are finite; a program needn't handle non-finite values.
Results may differ from a plain program's by a relative error of at most 0.0042.
Values may be sent and summed in bfloat16 or wider, within the bound.
A program may use at most 64 MiB of HBM per device.

v0:
```python
import math

import jax
import jax.numpy as jnp
from jax import lax
from jax.sharding import PartitionSpec as P

QUANT_LIMIT = 448.0
SCALE_FLOOR = 0.25


def quantize(values, scale):
    scaled = values.astype(jnp.float32) * scale
    return jnp.clip(scaled, -QUANT_LIMIT, QUANT_LIMIT).astype(jnp.bfloat16)


def place_peaks(history, peaks, slots):
    rows = lax.broadcasted_iota(jnp.int32, history.shape, 0)
    return jnp.where(rows == slots[None, :], peaks[None, :], history)


def body(activations, gradients, act_history, grad_history, owner_rank, history_slot):
    model_width = act_history.shape[2]
    column_total = gradients.shape[1]
    my_rank = lax.axis_index("tensor")
    held = jnp.where(owner_rank[None, :] == my_rank, act_history[0], jnp.float32(0.0))
    current_history = lax.psum(held, "tensor")
    act_scale = QUANT_LIMIT / jnp.maximum(jnp.max(current_history, axis=0), SCALE_FLOOR)
    grad_scale = QUANT_LIMIT / jnp.maximum(jnp.max(grad_history, axis=0), SCALE_FLOOR)
    grad_quant = quantize(gradients, grad_scale)
    row_count = model_width // lax.axis_size("dp")
    grad_factor = 1.0 / math.sqrt(gradients.shape[0] * lax.axis_size("dp"))
    own_act_peak = jnp.max(jnp.abs(activations), axis=0).astype(jnp.float32)
    own_grad_peak = jnp.max(jnp.abs(gradients), axis=0).astype(jnp.float32)
    contract_rows = (((0,), (0,)), ((), ()))
    act_source = quantize(activations, act_scale)
    gathered_rows = lax.all_gather(act_source, "tensor", axis=0, tiled=True)
    summed = lax.psum_scatter(
        lax.dot_general(
            gathered_rows, grad_quant, contract_rows, preferred_element_type=jnp.float32
        ),
        "dp",
        scatter_dimension=0,
        tiled=True,
    )
    act_peak = lax.pmax(own_act_peak, ("dp", "tensor"))
    grad_peak = lax.pmax(own_grad_peak, "dp")
    row_base = lax.axis_index("dp") * row_count
    row_scale = lax.dynamic_slice_in_dim(act_scale, row_base, row_count, 0)
    weight_grad = summed / (row_scale[:, None] * grad_scale[None, :]) * grad_factor
    act_slots = history_slot[:model_width]
    grad_slots = lax.dynamic_slice_in_dim(
        history_slot, model_width + my_rank * column_total, column_total, 0
    )
    updated = place_peaks(current_history, act_peak, act_slots)
    act_history_out = updated[None]
    grad_history_out = place_peaks(grad_history, grad_peak, grad_slots)
    return (weight_grad, act_history_out, grad_history_out)


def solution(mesh):
    placed = (
        P(("dp", "tensor"), None),
        P("dp", "tensor"),
        P("tensor", None, None),
        P(None, "tensor"),
        P(),
        P(),
    )
    return jax.shard_map(
        body,
        mesh=mesh,
        in_specs=placed,
        out_specs=(P("dp", "tensor"), P("tensor", None, None), P(None, "tensor")),
        check_vma=False,
    )
```

profile of v0, /device:TPU:0, one launch (start us, length us, event | category | flops | bytes accessed | tf_op | source)
XLA Modules:
  0.0 278.6 jit_solution(2231340872782706358)
XLA Ops:
  7.2 0.0 all-reduce.2.cloned.1.call-start
  7.2 0.7 broadcast_compare_fusion
  7.9 1.5 bitcast_select_fusion
  9.4 0.0 all-reduce.2.cloned.1.call-update
  9.4 0.0 all-gather.2.cloned.1.call-start
  9.5 1.8 abs_reduce_fusion.1
  11.3 0.7 slice.3
  12.0 41.9 %pmax.14 = f32[1024]{0:T(1024)S(1)} all-reduce(bf16[1024]{0:T(1024)(128)(2,1)S(1)} %abs_reduce_fusion.1), channel_id=1, replica_groups=mesh['dp'=16,'tensor'=2] {'dp','tensor'}, use_global_device_ids=true, to_apply=%region_5.6 | all-reduce | flops 1024 | bytes 6144 | tf_op jit(solution)/shard_map/pmax | solution.py:46
  53.9 0.0 all-reduce.2.cloned.1.call-done
  53.9 1.5 select_bitcast_fusion
  55.4 3.5 %clamp_convert_fusion.2 = bf16[1024,1024]{1,0:T(8,128)(2,1)} fusion(bf16[1024,1024]{1,0:T(8,128)(2,1)} %param.6, f32[1024]{0:T(1024)S(1)} %maximum_divide_fusion.1), kind=kLoop, calls=%fused_computation.6 | loop fusion | flops 4194304 | bytes 4198400 | tf_op jit(solution)/shard_map/convert_element_type | solution.py:14
  58.9 0.0 all-gather.2.cloned.1.call-update
  58.9 0.0 reduce-scatter.2.cloned.1.call-start
  59.0 0.8 dynamic_slice.7
  59.8 0.0 copy-start
  59.8 6.5 %abs_reduce_fusion = bf16[2736]{0:T(1024)(128)(2,1)S(1)} fusion(bf16[2048,2736]{0,1:T(8,128)(2,1)} %param.7), kind=kLoop, calls=%fused_computation.2 | loop fusion | flops 11203920 | bytes 11212128 | tf_op jit(solution)/shard_map/reduce_max | solution.py:34
  66.3 59.1 %pmax.15 = f32[2736]{0:T(1024)S(1)} all-reduce(bf16[2736]{0:T(1024)(128)(2,1)S(1)} %abs_reduce_fusion), channel_id=1, replica_groups=mesh['dp'=16,'tensor'=2] {'dp'}, use_global_device_ids=true, to_apply=%region_7.8 | all-reduce | flops 2736 | bytes 16416 | tf_op jit(solution)/shard_map/pmax | solution.py:47
  125.4 0.0 copy-done
  125.4 0.7 fusion.4
  126.1 0.0 all-gather.2.cloned.1.call-done
  126.1 19.3 %fusion = f32[1024,2736]{1,0:T(8,128)} fusion(bf16[2048,1024]{1,0:T(8,128)(2,1)} %all-gather.2.cloned.1.call-done, bf16[2048,2736]{0,1:T(8,128)(2,1)} %param.7, f32[2736]{0:T(1024)S(1)} %maximum_divide_fusion), kind=kOutput, calls=%fused_computation.1 | convolution fusion | flops 11498029056 | bytes 26618560 | tf_op jit(solution)/shard_map/dot_general | solution.py:39
  145.4 0.0 reduce-scatter.2.cloned.1.call-update
  145.5 0.1 dynamic_slice.6
  145.5 124.4 %reduce-scatter.2.cloned.1.call-done = f32[64,2736]{1,0:T(8,128)} async-done(((f32[1024,2736]{1,0:T(8,128)}), f32[64,2736]{1,0:T(8,128)}) %reduce-scatter.2.cloned.1.call-update) | async-done | bytes 700432 | tf_op jit(solution)/shard_map/reduce_scatter | solution.py:38
  269.9 2.1 divide_multiply_fusion
  (2 shorter events, 0.0 us)
Async XLA Ops:
  7.2 46.7 %all-reduce.2.cloned.1.call-start = ((), (), s32[]{:S(2)}) async-start(), calls=%async_computation.1 | async-start | bytes 131072 | tf_op jit(solution)/shard_map/psum | solution.py:27
  9.4 116.7 %all-gather.2.cloned.1.call-start = ((), (), s32[]{:S(2)}) async-start(), calls=%async_computation.2 | async-start | bytes 6291456 | tf_op jit(solution)/shard_map/all_gather | solution.py:37
  58.9 211.0 %reduce-scatter.2.cloned.1.call-start = ((), (), s32[]{:S(2)}) async-start(), calls=%async_computation.3 | async-start | bytes 12255232 | tf_op jit(solution)/shard_map/reduce_scatter | solution.py:38
  59.8 65.6 %copy-start = (f32[16,2736]{1,0:T(8,128)S(1)}, f32[16,2736]{1,0:T(8,128)}, u32[]{:S(2)}) copy-start(f32[16,2736]{1,0:T(8,128)} %param.9) | copy-start | bytes 525316
Sparse Core Ops, SparseCore 0:
  10.8 23.6 all-reduce.1
  59.1 56.5 all-gather.1
  145.6 124.2 reduce-scatter.1
where the time goes:
time: 279 us
  waiting for transfers between devices  124 us (44%)
  blocking collectives  101 us (36%)
  matrix products  19.3 us (7%)
  other arithmetic  18.4 us (7%)
  between operations  13.8 us (5%)
    reduce_scatter x1, waiting for transfers between devices, body(): lax.psum_scatter(lax.dot_general(gathered_rows, grad_quant, contract_rows...  124 us
    pmax x1, blocking collectives, body(): grad_peak = lax.pmax(own_grad_peak, 'dp')  59.1 us
    pmax x1, blocking collectives, body(): act_peak = lax.pmax(own_act_peak, ('dp', 'tensor'))  41.9 us
    dot_general x1, matrix products, body(): lax.dot_general(gathered_rows, grad_quant, contract_rows, preferred_eleme...  19.3 us
    reduce_max x1, other arithmetic, body(): own_grad_peak = jnp.max(jnp.abs(gradients), axis=0).astype(jnp.float32)  6.51 us
  transfers between devices with their start and end apart: 3, of which 1 were waited for; matrix products, arithmetic and copies ran while one was open for 4% of the time, Pallas kernels for 0%

commit v1 on v0

v1 whole, which is shorter than its diff:
```python
import functools
import math

import jax
import jax.numpy as jnp
from jax import lax
from jax.experimental import pallas as pl
from jax.experimental.pallas import tpu as pltpu
from jax.sharding import PartitionSpec as P

QUANT_LIMIT = 448.0
SCALE_FLOOR = 0.25
CORES = 2
ROWS_Y = 2
LANES = 128
COL_TILE = 512
MESH = pl.DeviceIdType.MESH


def quantize(values, scale):
    scaled = values.astype(jnp.float32) * scale
    return jnp.clip(scaled, -QUANT_LIMIT, QUANT_LIMIT).astype(jnp.bfloat16)


def place_peaks(history, peaks, slots):
    rows = lax.broadcasted_iota(jnp.int32, history.shape, 0)
    return jnp.where(rows == slots[None, :], peaks[None, :], history)


def col_tiles(width):
    return [(start, min(COL_TILE, width - start)) for start in range(0, width, COL_TILE)]


def fused_kernel(
    dp, tensor,
    act_hbm, grad_hbm, act_hist_ref, grad_hist_ref, owner_ref,
    summed_ref, cur_ref, act_peak_ref, grad_peak_ref,
    act_own, act_got, hist_got, gq, part, core_got, y_out, y_got, z_out, z_got,
    lhs, peaks, act_peaks, act_scale, grad_scale,
    load_sem, grad_sem, hist_send, hist_recv, x_send, x_recv, core_send, core_recv,
    y_send, y_recv, z_send, z_recv, pk_send, pk_recv, ap_send, ap_recv,
):
    me = lax.axis_index("dp")
    mt = lax.axis_index("tensor")
    core = lax.rem(me, CORES)
    chip = lax.div(me, CORES)
    yy = lax.rem(chip, ROWS_Y)
    zz = lax.div(chip, ROWS_Y)
    depth = dp // (CORES * ROWS_Y)
    tokens, width = act_hbm.shape
    rows, cols = grad_hbm.shape
    block = width // dp
    pair = block * CORES
    tiles = col_tiles(cols)
    load_rows = rows // grad_sem.shape[0]

    def dp_index(z, y, c):
        return (z * ROWS_Y + y) * CORES + c

    sibling = dp_index(zz, yy, 1 - core)
    y_peer = dp_index(zz, 1 - yy, core)

    def grad_load(i):
        at = pl.ds(pl.multiple_of(i * load_rows, load_rows), load_rows)
        return pltpu.make_async_copy(grad_hbm.at[at], gq.at[at], grad_sem.at[i])

    def start_load(i, carry):
        grad_load(i).start()
        return carry

    act_load = pltpu.make_async_copy(act_hbm, act_own, load_sem)
    act_load.start()
    lax.fori_loop(0, grad_sem.shape[0], start_load, 0)

    barrier = pltpu.get_barrier_semaphore()
    for t in range(1, tensor):
        pl.semaphore_signal(
            barrier, inc=1, device_id={"tensor": lax.rem(mt + t, tensor)}, device_id_type=MESH
        )

    def greet(k, carry):
        pl.semaphore_signal(
            barrier, inc=1, device_id={"dp": lax.rem(me + k, dp)}, device_id_type=MESH
        )
        return carry

    lax.fori_loop(1, dp, greet, 0)
    pl.semaphore_wait(barrier, dp - 1 + tensor - 1)

    def target_z(u):
        return lax.rem(zz + 1 + u, depth)

    def block_cols(u, k):
        y = 1 - yy if k == 0 else yy
        return pl.ds(pl.multiple_of((target_z(u) * ROWS_Y + y) * pair, LANES), pair)

    def hist_copy(t):
        return pltpu.make_async_remote_copy(
            src_ref=act_hist_ref.at[0], dst_ref=hist_got.at[t - 1],
            send_sem=hist_send.at[t - 1], recv_sem=hist_recv.at[t - 1],
            device_id={"tensor": lax.rem(mt + t, tensor)}, device_id_type=MESH,
        )

    def x_copy(t, u, k):
        at = block_cols(u, k)
        return pltpu.make_async_remote_copy(
            src_ref=act_hbm.at[:, at], dst_ref=act_got.at[t - 1, :, at],
            send_sem=x_send.at[t - 1, u * 2 + k], recv_sem=x_recv.at[t - 1, u * 2 + k],
            device_id={"tensor": lax.rem(mt + t, tensor)}, device_id_type=MESH,
        )

    def core_copy(s):
        return pltpu.make_async_remote_copy(
            src_ref=part.at[s, pl.ds(pl.multiple_of((1 - core) * block, block), block)],
            dst_ref=core_got.at[s],
            send_sem=core_send.at[s], recv_sem=core_recv.at[s],
            device_id={"dp": sibling}, device_id_type=MESH,
        )

    def y_copy(u):
        return pltpu.make_async_remote_copy(
            src_ref=y_out.at[u], dst_ref=y_got.at[u],
            send_sem=y_send.at[u], recv_sem=y_recv.at[u],
            device_id={"dp": y_peer}, device_id_type=MESH,
        )

    def z_copy(u):
        return pltpu.make_async_remote_copy(
            src_ref=z_out.at[u], dst_ref=z_got.at[u],
            send_sem=z_send.at[u], recv_sem=z_recv.at[u],
            device_id={"dp": dp_index(target_z(u), yy, core)}, device_id_type=MESH,
        )

    def peak_copy(k):
        return pltpu.make_async_remote_copy(
            src_ref=peaks.at[0], dst_ref=peaks.at[k],
            send_sem=pk_send.at[k - 1], recv_sem=pk_recv.at[k - 1],
            device_id={"dp": lax.rem(me + k, dp)}, device_id_type=MESH,
        )

    def act_peak_copy(t):
        return pltpu.make_async_remote_copy(
            src_ref=act_peaks.at[0], dst_ref=act_peaks.at[t],
            send_sem=ap_send.at[t - 1], recv_sem=ap_recv.at[t - 1],
            device_id={"tensor": lax.rem(mt + t, tensor)}, device_id_type=MESH,
        )

    for t in range(1, tensor):
        hist_copy(t).start()

    def start_x(u, carry):
        for k in range(2):
            for t in range(1, tensor):
                x_copy(t, u, k).start()
        return carry

    lax.fori_loop(0, depth, start_x, 0)

    grad_scale[...] = QUANT_LIMIT / jnp.maximum(
        jnp.max(grad_hist_ref[...], axis=0, keepdims=True), SCALE_FLOOR
    )

    act_load.wait()
    step_rows = min(64, tokens)
    for start, size in col_tiles(width):
        def peak_rows(r, top, start=start, size=size):
            at = pl.ds(pl.multiple_of(r * step_rows, step_rows), step_rows)
            mag = jnp.abs(act_own[at, start:start + size])
            return jnp.maximum(top, jnp.max(mag.reshape(step_rows // 16, 16, size), axis=0))

        top = lax.fori_loop(
            0, tokens // step_rows, peak_rows, jnp.zeros((16, size), jnp.bfloat16)
        )
        peaks[0, :, start:start + size] = jnp.max(
            top.astype(jnp.float32), axis=0, keepdims=True
        )
    peaks[0, :, width:] = jnp.zeros((1, cols), jnp.float32)

    def grad_chunk(i, carry):
        grad_load(i).wait()
        for start, size in tiles:
            scale = grad_scale[:, start:start + size]

            def quant_rows(r, top, start=start, size=size, scale=scale):
                at = pl.ds(
                    pl.multiple_of(i * load_rows + r * step_rows, step_rows), step_rows
                )
                raw = gq[at, start:start + size]
                mag = jnp.abs(raw)
                gq[at, start:start + size] = quantize(raw, scale)
                return jnp.maximum(top, jnp.max(mag.reshape(step_rows // 16, 16, size), axis=0))

            top = lax.fori_loop(
                0, load_rows // step_rows, quant_rows, jnp.zeros((16, size), jnp.bfloat16)
            )
            here = slice(width + start, width + start + size)
            peaks[0, :, here] = jnp.maximum(
                peaks[0, :, here], jnp.max(top.astype(jnp.float32), axis=0, keepdims=True)
            )
        return carry

    lax.fori_loop(0, grad_sem.shape[0], grad_chunk, 0)

    def start_peak(k, carry):
        peak_copy(k).start()
        return carry

    lax.fori_loop(1, dp, start_peak, 0)

    owner = owner_ref[...]
    current = jnp.where(owner == mt, act_hist_ref[0], 0.0)
    for t in range(1, tensor):
        hist_copy(t).wait()
        source = lax.rem(mt + tensor - t, tensor)
        current = jnp.where(owner == source, hist_got[t - 1], current)
    cur_ref[...] = current
    act_scale[...] = QUANT_LIMIT / jnp.maximum(
        jnp.max(current, axis=0, keepdims=True), SCALE_FLOOR
    )

    def load_lhs(read, at):
        scaled = read.astype(jnp.float32) * act_scale[:, at]
        scaled = jnp.clip(scaled, -QUANT_LIMIT, QUANT_LIMIT)
        lhs[...] = jnp.transpose(scaled).astype(jnp.bfloat16)

    def multiply(s, source, first):
        at = pl.ds(pl.multiple_of(source * tokens, tokens), tokens)
        full = cols // COL_TILE

        def one(start, size):
            here = pl.ds(start, size)
            term = jnp.dot(lhs[...], gq[at, here], preferred_element_type=jnp.float32)
            if first:
                part[s, :, here] = term
            else:
                part[s, :, here] += term

        def tile(j, carry):
            one(pl.multiple_of(j * COL_TILE, COL_TILE), COL_TILE)
            return carry

        lax.fori_loop(0, full, tile, 0)
        if cols % COL_TILE:
            one(full * COL_TILE, cols % COL_TILE)

    mine = pl.ds(pl.multiple_of(core * block, block), block)

    def block_step(u, k):
        s = u * 2 + k
        at = block_cols(u, k)
        load_lhs(act_own[:, at], at)
        multiply(s, mt, True)
        for t in range(1, tensor):
            x_copy(t, u, k).wait_recv()
            load_lhs(act_got[t - 1, :, at], at)
            multiply(s, lax.rem(mt + tensor - t, tensor), False)
        core_copy(s).start()
        core_copy(s).wait_recv()
        both = part[s, mine, :] + core_got[s]
        if k == 0:
            y_out[u] = both.astype(jnp.bfloat16)
            y_copy(u).start()
        else:
            part[s, mine, :] = both

    def send_z(u):
        y_copy(u).wait_recv()
        z_out[u] = (part[u * 2 + 1, mine, :] + y_got[u].astype(jnp.float32)).astype(jnp.bfloat16)
        z_copy(u).start()

    def unit(u, carry):
        block_step(u, 0)

        @pl.when(u >= 1)
        def _():
            send_z(u - 1)

        block_step(u, 1)
        return carry

    lax.fori_loop(0, depth, unit, 0)

    def wait_peak(k, carry):
        peak_copy(k).wait()
        return carry

    lax.fori_loop(1, dp, wait_peak, 0)
    tops = jnp.max(peaks[...], axis=0)
    grad_peak_ref[...] = tops[:, width:]
    act_peaks[0] = tops[:, :width]
    for t in range(1, tensor):
        act_peak_copy(t).start()

    y_copy(depth - 1).wait_recv()
    total = part[depth * 2 - 1, mine, :] + y_got[depth - 1].astype(jnp.float32)
    for u in range(depth - 1):
        z_copy(u).wait_recv()
        total = total + z_got[u].astype(jnp.float32)
    summed_ref[...] = total

    for t in range(1, tensor):
        act_peak_copy(t).wait()
    act_peak_ref[...] = jnp.max(act_peaks[...], axis=0)

    def finish(u, carry):
        for k in range(2):
            for t in range(1, tensor):
                x_copy(t, u, k).wait_send()
            core_copy(u * 2 + k).wait_send()
        y_copy(u).wait_send()
        return carry

    lax.fori_loop(0, depth, finish, 0)

    def finish_z(u, carry):
        z_copy(u).wait_send()
        return carry

    lax.fori_loop(0, depth - 1, finish_z, 0)


def fused_sums(activations, gradients, act_history, grad_history, owner_rank):
    dp, tensor = lax.axis_size("dp"), lax.axis_size("tensor")
    tokens, width = activations.shape
    rows, cols = gradients.shape
    hist = act_history.shape[1]
    depth = dp // (CORES * ROWS_Y)
    steps = depth * ROWS_Y
    block = width // dp
    loads = 8
    dma = pltpu.SemaphoreType.DMA
    vmem = pl.BlockSpec(memory_space=pltpu.VMEM)
    hbm = pl.BlockSpec(memory_space=pl.ANY)
    f32, bf16 = jnp.float32, jnp.bfloat16
    others = tensor - 1
    return pl.pallas_call(
        functools.partial(fused_kernel, dp, tensor),
        out_shape=(
            jax.ShapeDtypeStruct((block, cols), f32),
            jax.ShapeDtypeStruct((hist, width), f32),
            jax.ShapeDtypeStruct((1, width), f32),
            jax.ShapeDtypeStruct((1, cols), f32),
        ),
        in_specs=[hbm, hbm, vmem, vmem, vmem],
        out_specs=(vmem, vmem, vmem, vmem),
        scratch_shapes=[
            pltpu.VMEM((tokens, width), bf16),
            pltpu.VMEM((others, tokens, width), bf16),
            pltpu.VMEM((others, hist, width), f32),
            pltpu.VMEM((rows, cols), bf16),
            pltpu.VMEM((steps, block * CORES, cols), f32),
            pltpu.VMEM((steps, block, cols), f32),
            pltpu.VMEM((depth, block, cols), bf16),
            pltpu.VMEM((depth, block, cols), bf16),
            pltpu.VMEM((depth, block, cols), bf16),
            pltpu.VMEM((depth, block, cols), bf16),
            pltpu.VMEM((block * CORES, tokens), bf16),
            pltpu.VMEM((dp, 1, width + cols), f32),
            pltpu.VMEM((tensor, 1, width), f32),
            pltpu.VMEM((1, width), f32),
            pltpu.VMEM((1, cols), f32),
            dma, dma((loads,)), dma((others,)), dma((others,)),
            dma((others, steps)), dma((others, steps)), dma((steps,)), dma((steps,)),
            dma((depth,)), dma((depth,)), dma((depth,)), dma((depth,)),
            dma((dp - 1,)), dma((dp - 1,)), dma((others,)), dma((others,)),
        ],
        compiler_params=pltpu.CompilerParams(
            collective_id=0, has_side_effects=True, vmem_limit_bytes=60 * 1024 * 1024
        ),
    )(activations, gradients, act_history, grad_history, owner_rank[None, :])


def gathered_sums(activations, gradients, act_history, grad_history, owner_rank):
    my_rank = lax.axis_index("tensor")
    held = jnp.where(owner_rank[None, :] == my_rank, act_history[0], jnp.float32(0.0))
    current = lax.psum(held, "tensor")
    act_scale = QUANT_LIMIT / jnp.maximum(jnp.max(current, axis=0), SCALE_FLOOR)
    grad_scale = QUANT_LIMIT / jnp.maximum(jnp.max(grad_history, axis=0), SCALE_FLOOR)
    gathered_rows = lax.all_gather(quantize(activations, act_scale), "tensor", axis=0, tiled=True)
    summed = lax.psum_scatter(
        lax.dot_general(
            gathered_rows, quantize(gradients, grad_scale), (((0,), (0,)), ((), ())),
            preferred_element_type=jnp.float32,
        ),
        "dp", scatter_dimension=0, tiled=True,
    )
    act_peak = lax.pmax(jnp.max(jnp.abs(activations), axis=0).astype(jnp.float32), ("dp", "tensor"))
    grad_peak = lax.pmax(jnp.max(jnp.abs(gradients), axis=0).astype(jnp.float32), "dp")
    return summed, current, act_peak[None, :], grad_peak[None, :]


def body(activations, gradients, act_history, grad_history, owner_rank, history_slot):
    dp = lax.axis_size("dp")
    model_width = act_history.shape[2]
    column_total = gradients.shape[1]
    row_count = model_width // dp
    fits = dp % (CORES * ROWS_Y) == 0 and (row_count * CORES) % LANES == 0
    sums = fused_sums if fits else gathered_sums
    summed, current, act_peak, grad_peak = sums(
        activations, gradients, act_history, grad_history, owner_rank
    )
    act_scale = QUANT_LIMIT / jnp.maximum(jnp.max(current, axis=0), SCALE_FLOOR)
    grad_scale = QUANT_LIMIT / jnp.maximum(jnp.max(grad_history, axis=0), SCALE_FLOOR)
    grad_factor = 1.0 / math.sqrt(gradients.shape[0] * dp)
    row_base = lax.axis_index("dp") * row_count
    row_scale = lax.dynamic_slice_in_dim(act_scale, row_base, row_count, 0)
    weight_grad = summed / (row_scale[:, None] * grad_scale[None, :]) * grad_factor
    act_slots = history_slot[:model_width]
    grad_slots = lax.dynamic_slice_in_dim(
        history_slot, model_width + lax.axis_index("tensor") * column_total, column_total, 0
    )
    act_history_out = place_peaks(current, act_peak[0], act_slots)[None]
    grad_history_out = place_peaks(grad_history, grad_peak[0], grad_slots)
    return (weight_grad, act_history_out, grad_history_out)


def solution(mesh):
    placed = (
        P(("dp", "tensor"), None),
        P("dp", "tensor"),
        P("tensor", None, None),
        P(None, "tensor"),
        P(),
        P(),
    )
    return jax.shard_map(
        body,
        mesh=mesh,
        in_specs=placed,
        out_specs=(P("dp", "tensor"), P("tensor", None, None), P(None, "tensor")),
        check_vma=False,
    )
```

time: 279 us -> 93.4 us (0.33)
  waiting for transfers between devices: 124 us -> 0 us
  blocking collectives: 101 us -> 0 us
  Pallas kernels: 0 us -> 71.4 us
  matrix products: 19.3 us -> 0 us
  local copies, waits for them, and re-layouts: 1.57 us -> 15.6 us
  other arithmetic: 18.4 us -> 5.08 us
  between operations: 13.8 us -> 0.66 us
    reduce_scatter x1 -> x0, waiting for transfers between devices: 124 us -> none  [body(): lax.psum_scatter(lax.dot_general(gathered_rows, grad_quant, contract_rows...]
    pmax x2 -> x0, blocking collectives: 101 us -> none  [the longest x1 59.1 us: body(): grad_peak = lax.pmax(own_grad_peak, 'dp')]
    pallas_call x0 -> x1, Pallas kernels: none -> 71.4 us  [fused_sums(): pl.pallas_call(functools.partial(fused_kernel, dp, tensor), out_shape=(ja...]
    dot_general x1 -> x0, matrix products: 19.3 us -> none  [body(): lax.dot_general(gathered_rows, grad_quant, contract_rows, preferred_eleme...]
    unnamed x2 -> x5, local copies, waits for them, and re-layouts: 0.01 us -> 15.5 us
    reduce_max x2 -> x0, other arithmetic: 8.33 us -> none  [the longest x1 6.51 us: body(): own_grad_peak = jnp.max(jnp.abs(gradients), axis=0).astype(jnp.float32)]
    convert_element_type x1 -> x0, other arithmetic: 3.53 us -> none  [quantize(): return jnp.clip(scaled, -QUANT_LIMIT, QUANT_LIMIT).astype(jnp.bfloat16)]
  transfers between devices with their start and end apart: 3 -> 0, of which waited for: 1 -> 0; matrix products, arithmetic and copies ran while one was open for 4% -> 0% of each run, Pallas kernels for 0% -> 0%
where the time goes in v1:
time: 93.4 us; the launch traced here: 92.8 us
  Pallas kernels  71.4 us (76%)
  local copies, waits for them, and re-layouts  15.6 us (17%)
  other arithmetic  5.08 us (5%)
    pallas_call x1, Pallas kernels, fused_sums(): pl.pallas_call(functools.partial(fused_kernel, dp, tensor), out_shape=(ja...  71.4 us
    unnamed x5, local copies, waits for them, and re-layouts  15.5 us
    mul x1, other arithmetic, body(): summed / (row_scale[:, None] * grad_scale[None, :]) * grad_factor  2.15 us

profile of v1, /device:TPU:0, one launch (start us, length us, event | category | flops | bytes accessed | tf_op | source)
XLA Modules:
  0.0 92.8 jit_solution(16290507202605206616)
XLA Ops:
  0.6 15.5 %copy.9.grad_hbm = bf16[2048,2736]{1,0:T(8,128)(2,1)} copy(bf16[2048,2736]{0,1:T(8,128)(2,1)} %param.7) | data formatting | bytes 22413312 | tf_op args[1]
  16.1 0.0 copy-start.1
  16.1 0.0 copy-start
  16.1 0.0 slice-start
  16.1 71.4 %shard_map.85 = (f32[64,2736]{1,0:T(8,128)}, f32[16,1024]{1,0:T(8,128)}, f32[1,1024]{1,0:T(1,128)}, f32[1,2736]{1,0:T(1,128)}) custom-call(bf16[1024,1024]{1,0:T(8,128)(2,1)} %act_hbm.1, bf16[2048,2736]{1,0:T(8,128)(2,1)} %copy.9.grad_hbm, f32[1,16,1024]{2,1,0:T(8,128)} %act_hist_ref.1, f32[16,2736]{1,0:T(8,128)} %grad_hist_ref.1, s32[1,1024]{1,0:T(1,128)} %bitcast.4), custom_call_target="tpu_custom_call" | custom-call | tf_op jit(solution)/shard_map/pallas_call | solution.py:336
  87.5 0.7 reduce
  88.3 0.0 copy-done.1
  88.3 0.1 dynamic_slice.7
  88.4 0.0 copy-done
  88.4 0.7 fusion
  89.1 0.0 slice-done
  89.1 1.5 %select_bitcast_fusion = (f32[1,16,1024]{2,1,0:T(8,128)}, f32[1024]{0:T(1024)S(1)}) fusion(f32[16,1024]{1,0:T(8,128)} %get-tuple-element.8, f32[1024]{0:T(1024)} %bitcast.5, s32[1024]{0:T(1024)S(1)} %slice-done), kind=kLoop, calls=%fused_computation.3 | loop fusion | flops 48128 | bytes 143360 | tf_op jit(solution)/shard_map/broadcast_in_dim | solution.py:412
  90.6 0.1 dynamic_slice.6
  90.6 2.1 %divide_multiply_fusion = f32[64,2736]{1,0:T(8,128)} fusion(f32[64,2736]{1,0:T(8,128)} %get-tuple-element.7, f32[2736]{0:T(1024)S(1)} %maximum_divide_fusion, f32[64]{0:T(128)S(1)} %dynamic_slice.6), kind=kLoop, calls=%fused_computation | loop fusion | flops 525312 | bytes 1412032 | tf_op jit(solution)/shard_map/mul | solution.py:407
  (2 shorter events, 0.0 us)
Async XLA Ops:
  16.1 72.2 %copy-start.1 = (s32[6496]{0:T(1024)S(1)}, s32[6496]{0:T(1024)}, u32[]{:S(2)}) copy-start(s32[6496]{0:T(1024)} %param.11) | copy-start | bytes 77956
  16.1 72.3 %copy-start = (f32[16,2736]{1,0:T(8,128)S(1)}, f32[16,2736]{1,0:T(8,128)}, u32[]{:S(2)}) copy-start(f32[16,2736]{1,0:T(8,128)} %grad_hist_ref.1) | copy-start | bytes 525316
  16.1 73.0 %slice-start = ((s32[6496]{0:T(1024)}), s32[1024]{0:T(1024)S(1)}, s32[]{:S(2)}) async-start(s32[6496]{0:T(1024)} %param.11), calls=%async_computation | async-start | bytes 8192 | tf_op jit(solution)/shard_map/slice | solution.py:408

commit v2 on v1

--- a/solution.py
+++ b/solution.py
@@ -13,6 +13,7 @@
 CORES = 2
 ROWS_Y = 2
 LANES = 128
+SUBLANES = 16
 COL_TILE = 512
 MESH = pl.DeviceIdType.MESH
 
@@ -33,10 +34,10 @@
 
 def fused_kernel(
     dp, tensor,
-    act_hbm, grad_hbm, act_hist_ref, grad_hist_ref, owner_ref,
-    summed_ref, cur_ref, act_peak_ref, grad_peak_ref,
+    act_hbm, grad_hbm, act_hist_ref, grad_hist_ref, owner_ref, act_slot_ref, grad_slot_ref,
+    weight_ref, act_hist_out, grad_hist_out,
     act_own, act_got, hist_got, gq, part, core_got, y_out, y_got, z_out, z_got,
-    lhs, peaks, act_peaks, act_scale, grad_scale,
+    lhs, peaks, act_peaks, act_scale, grad_scale, scale_down, peak_down, row_undo, current_hist,
     load_sem, grad_sem, hist_send, hist_recv, x_send, x_recv, core_send, core_recv,
     y_send, y_recv, z_send, z_recv, pk_send, pk_recv, ap_send, ap_recv,
 ):
@@ -48,11 +49,11 @@
     zz = lax.div(chip, ROWS_Y)
     depth = dp // (CORES * ROWS_Y)
     tokens, width = act_hbm.shape
-    rows, cols = grad_hbm.shape
+    cols, rows = grad_hbm.shape
     block = width // dp
     pair = block * CORES
-    tiles = col_tiles(cols)
-    load_rows = rows // grad_sem.shape[0]
+    load_cols = cols // grad_sem.shape[0]
+    padded = grad_scale.shape[1]
 
     def dp_index(z, y, c):
         return (z * ROWS_Y + y) * CORES + c
@@ -61,7 +62,7 @@
     y_peer = dp_index(zz, 1 - yy, core)
 
     def grad_load(i):
-        at = pl.ds(pl.multiple_of(i * load_rows, load_rows), load_rows)
+        at = pl.ds(pl.multiple_of(i * load_cols, SUBLANES), load_cols)
         return pltpu.make_async_copy(grad_hbm.at[at], gq.at[at], grad_sem.at[i])
 
     def start_load(i, carry):
@@ -91,7 +92,7 @@
         return lax.rem(zz + 1 + u, depth)
 
     def block_cols(u, k):
-        y = 1 - yy if k == 0 else yy
+        y = yy * k + (1 - yy) * (1 - k)
         return pl.ds(pl.multiple_of((target_z(u) * ROWS_Y + y) * pair, LANES), pair)
 
     def hist_copy(t):
@@ -148,17 +149,31 @@
     for t in range(1, tensor):
         hist_copy(t).start()
 
-    def start_x(u, carry):
-        for k in range(2):
-            for t in range(1, tensor):
-                x_copy(t, u, k).start()
-        return carry
-
-    lax.fori_loop(0, depth, start_x, 0)
-
-    grad_scale[...] = QUANT_LIMIT / jnp.maximum(
+    def send_x(u, k):
+        for t in range(1, tensor):
+            x_copy(t, u, k).start()
+
+    def send_pair(u, carry):
+        send_x(u + 1, 0)
+        send_x(u, 1)
+        return carry
+
+    send_x(0, 0)
+    lax.fori_loop(0, depth - 1, send_pair, 0)
+    send_x(depth - 1, 1)
+
+    grad_scale[:, padded - LANES:] = jnp.ones((1, LANES), jnp.float32)
+    grad_scale[:, :cols] = QUANT_LIMIT / jnp.maximum(
         jnp.max(grad_hist_ref[...], axis=0, keepdims=True), SCALE_FLOOR
     )
+    peak_down[padded - LANES:, :] = jnp.zeros((LANES, LANES), jnp.float32)
+
+    def turn_scale(j, carry):
+        at = pl.ds(pl.multiple_of(j * LANES, LANES), LANES)
+        scale_down[at, :] = jnp.transpose(jnp.broadcast_to(grad_scale[:, at], (LANES, LANES)))
+        return carry
+
+    lax.fori_loop(0, padded // LANES, turn_scale, 0)
 
     act_load.wait()
     step_rows = min(64, tokens)
@@ -174,32 +189,32 @@
         peaks[0, :, start:start + size] = jnp.max(
             top.astype(jnp.float32), axis=0, keepdims=True
         )
-    peaks[0, :, width:] = jnp.zeros((1, cols), jnp.float32)
-
     def grad_chunk(i, carry):
         grad_load(i).wait()
-        for start, size in tiles:
-            scale = grad_scale[:, start:start + size]
-
-            def quant_rows(r, top, start=start, size=size, scale=scale):
-                at = pl.ds(
-                    pl.multiple_of(i * load_rows + r * step_rows, step_rows), step_rows
-                )
-                raw = gq[at, start:start + size]
-                mag = jnp.abs(raw)
-                gq[at, start:start + size] = quantize(raw, scale)
-                return jnp.maximum(top, jnp.max(mag.reshape(step_rows // 16, 16, size), axis=0))
-
-            top = lax.fori_loop(
-                0, load_rows // step_rows, quant_rows, jnp.zeros((16, size), jnp.bfloat16)
-            )
-            here = slice(width + start, width + start + size)
-            peaks[0, :, here] = jnp.maximum(
-                peaks[0, :, here], jnp.max(top.astype(jnp.float32), axis=0, keepdims=True)
-            )
-        return carry
+
+        def quant_cols(j, inner):
+            at = pl.ds(pl.multiple_of(i * load_cols + j * SUBLANES, SUBLANES), SUBLANES)
+            scale = scale_down[at, :]
+            top = jnp.zeros((SUBLANES, LANES), jnp.bfloat16)
+            for start in range(0, rows, LANES):
+                raw = gq[at, start:start + LANES]
+                top = jnp.maximum(top, jnp.abs(raw))
+                gq[at, start:start + LANES] = quantize(raw, scale)
+            peak_down[at, :] = top.astype(jnp.float32)
+            return inner
+
+        return lax.fori_loop(0, load_cols // SUBLANES, quant_cols, carry)
 
     lax.fori_loop(0, grad_sem.shape[0], grad_chunk, 0)
+
+    def turn_peak(j, carry):
+        at = pl.ds(pl.multiple_of(j * LANES, LANES), LANES)
+        turned = jnp.transpose(peak_down[at, :])
+        here = pl.ds(pl.multiple_of(width + j * LANES, LANES), LANES)
+        peaks[0, :, here] = jnp.max(turned, axis=0, keepdims=True)
+        return carry
+
+    lax.fori_loop(0, padded // LANES, turn_peak, 0)
 
     def start_peak(k, carry):
         peak_copy(k).start()
@@ -213,7 +228,7 @@
         hist_copy(t).wait()
         source = lax.rem(mt + tensor - t, tensor)
         current = jnp.where(owner == source, hist_got[t - 1], current)
-    cur_ref[...] = current
+    current_hist[...] = current
     act_scale[...] = QUANT_LIMIT / jnp.maximum(
         jnp.max(current, axis=0, keepdims=True), SCALE_FLOOR
     )
@@ -229,7 +244,10 @@
 
         def one(start, size):
             here = pl.ds(start, size)
-            term = jnp.dot(lhs[...], gq[at, here], preferred_element_type=jnp.float32)
+            term = lax.dot_general(
+                lhs[...], gq[here, at], (((1,), (1,)), ((), ())),
+                preferred_element_type=jnp.float32,
+            )
             if first:
                 part[s, :, here] = term
             else:
@@ -245,40 +263,48 @@
 
     mine = pl.ds(pl.multiple_of(core * block, block), block)
 
-    def block_step(u, k):
-        s = u * 2 + k
+    def own_product(u, k):
         at = block_cols(u, k)
         load_lhs(act_own[:, at], at)
-        multiply(s, mt, True)
+        multiply(u * 2 + k, mt, True)
+
+    def got_product(u, k):
+        at = block_cols(u, k)
         for t in range(1, tensor):
             x_copy(t, u, k).wait_recv()
             load_lhs(act_got[t - 1, :, at], at)
-            multiply(s, lax.rem(mt + tensor - t, tensor), False)
-        core_copy(s).start()
-        core_copy(s).wait_recv()
-        both = part[s, mine, :] + core_got[s]
-        if k == 0:
-            y_out[u] = both.astype(jnp.bfloat16)
-            y_copy(u).start()
-        else:
-            part[s, mine, :] = both
-
-    def send_z(u):
+            multiply(u * 2 + k, lax.rem(mt + tensor - t, tensor), False)
+        core_copy(u * 2 + k).start()
+
+    def core_sum(u, k):
+        core_copy(u * 2 + k).wait_recv()
+        return part[u * 2 + k, mine, :] + core_got[u * 2 + k]
+
+    def send_y(u):
+        y_out[u] = core_sum(u, 0).astype(jnp.bfloat16)
+        y_copy(u).start()
+
+    def line_sum(u):
         y_copy(u).wait_recv()
-        z_out[u] = (part[u * 2 + 1, mine, :] + y_got[u].astype(jnp.float32)).astype(jnp.bfloat16)
+        return core_sum(u, 1) + y_got[u].astype(jnp.float32)
+
+    own_product(0, 0)
+    got_product(0, 0)
+    own_product(*((1, 0) if depth > 1 else (0, 1)))
+    send_y(0)
+
+    def unit(u, carry):
+        got_product(u + 1, 0)
+        own_product(u, 1)
+        send_y(u + 1)
+        got_product(u, 1)
+        last = lax.div(u + 2, depth)
+        own_product(u + 2 - last, last)
+        z_out[u] = line_sum(u).astype(jnp.bfloat16)
         z_copy(u).start()
-
-    def unit(u, carry):
-        block_step(u, 0)
-
-        @pl.when(u >= 1)
-        def _():
-            send_z(u - 1)
-
-        block_step(u, 1)
-        return carry
-
-    lax.fori_loop(0, depth, unit, 0)
+        return carry
+
+    lax.fori_loop(0, depth - 1, unit, 0)
 
     def wait_peak(k, carry):
         peak_copy(k).wait()
@@ -286,21 +312,35 @@
 
     lax.fori_loop(1, dp, wait_peak, 0)
     tops = jnp.max(peaks[...], axis=0)
-    grad_peak_ref[...] = tops[:, width:]
     act_peaks[0] = tops[:, :width]
     for t in range(1, tensor):
         act_peak_copy(t).start()
-
-    y_copy(depth - 1).wait_recv()
-    total = part[depth * 2 - 1, mine, :] + y_got[depth - 1].astype(jnp.float32)
+    hist_row = lax.broadcasted_iota(jnp.int32, grad_hist_ref.shape, 0)
+    grad_hist_out[...] = jnp.where(
+        hist_row == grad_slot_ref[...], tops[:, width:width + cols], grad_hist_ref[...]
+    )
+
+    picks = lax.broadcasted_iota(jnp.int32, (block, width), 1) == (
+        lax.broadcasted_iota(jnp.int32, (block, width), 0) + me * block
+    )
+    row_scale = jnp.sum(jnp.where(picks, act_scale[...], 0.0), axis=1, keepdims=True)
+    row_undo[...] = jnp.broadcast_to(1.0 / row_scale, row_undo.shape)
+    factor = 1.0 / math.sqrt(rows * dp)
+    grad_scale[...] = factor / grad_scale[...]
+
+    for t in range(1, tensor):
+        act_peak_copy(t).wait()
+    hist_row = lax.broadcasted_iota(jnp.int32, current_hist.shape, 0)
+    act_hist_out[0] = jnp.where(
+        hist_row == act_slot_ref[...], jnp.max(act_peaks[...], axis=0), current_hist[...]
+    )
+
+    got_product(depth - 1, 1)
+    total = line_sum(depth - 1)
     for u in range(depth - 1):
         z_copy(u).wait_recv()
         total = total + z_got[u].astype(jnp.float32)
-    summed_ref[...] = total
-
-    for t in range(1, tensor):
-        act_peak_copy(t).wait()
-    act_peak_ref[...] = jnp.max(act_peaks[...], axis=0)
+    weight_ref[...] = total * row_undo[:, :1] * grad_scale[:, :cols]
 
     def finish(u, carry):
         for k in range(2):
@@ -319,7 +359,7 @@
     lax.fori_loop(0, depth - 1, finish_z, 0)
 
 
-def fused_sums(activations, gradients, act_history, grad_history, owner_rank):
+def fused_outputs(activations, gradients, act_history, grad_history, owner_rank, act_slots, grad_slots):
     dp, tensor = lax.axis_size("dp"), lax.axis_size("tensor")
     tokens, width = activations.shape
     rows, cols = gradients.shape
@@ -327,7 +367,8 @@
     depth = dp // (CORES * ROWS_Y)
     steps = depth * ROWS_Y
     block = width // dp
-    loads = 8
+    loads = max(n for n in range(1, 13) if (cols // SUBLANES) % n == 0)
+    padded = pl.cdiv(cols, LANES) * LANES
     dma = pltpu.SemaphoreType.DMA
     vmem = pl.BlockSpec(memory_space=pltpu.VMEM)
     hbm = pl.BlockSpec(memory_space=pl.ANY)
@@ -337,17 +378,16 @@
         functools.partial(fused_kernel, dp, tensor),
         out_shape=(
             jax.ShapeDtypeStruct((block, cols), f32),
-            jax.ShapeDtypeStruct((hist, width), f32),
-            jax.ShapeDtypeStruct((1, width), f32),
-            jax.ShapeDtypeStruct((1, cols), f32),
+            jax.ShapeDtypeStruct((1, hist, width), f32),
+            jax.ShapeDtypeStruct((hist, cols), f32),
         ),
-        in_specs=[hbm, hbm, vmem, vmem, vmem],
-        out_specs=(vmem, vmem, vmem, vmem),
+        in_specs=[hbm, hbm, vmem, vmem, vmem, vmem, vmem],
+        out_specs=(vmem, vmem, vmem),
         scratch_shapes=[
             pltpu.VMEM((tokens, width), bf16),
             pltpu.VMEM((others, tokens, width), bf16),
             pltpu.VMEM((others, hist, width), f32),
-            pltpu.VMEM((rows, cols), bf16),
+            pltpu.VMEM((cols, rows), bf16),
             pltpu.VMEM((steps, block * CORES, cols), f32),
             pltpu.VMEM((steps, block, cols), f32),
             pltpu.VMEM((depth, block, cols), bf16),
@@ -355,10 +395,14 @@
             pltpu.VMEM((depth, block, cols), bf16),
             pltpu.VMEM((depth, block, cols), bf16),
             pltpu.VMEM((block * CORES, tokens), bf16),
-            pltpu.VMEM((dp, 1, width + cols), f32),
+            pltpu.VMEM((dp, 1, width + padded), f32),
             pltpu.VMEM((tensor, 1, width), f32),
             pltpu.VMEM((1, width), f32),
-            pltpu.VMEM((1, cols), f32),
+            pltpu.VMEM((1, padded), f32),
+            pltpu.VMEM((padded, LANES), f32),
+            pltpu.VMEM((padded, LANES), f32),
+            pltpu.VMEM((block, LANES), f32),
+            pltpu.VMEM((hist, width), f32),
             dma, dma((loads,)), dma((others,)), dma((others,)),
             dma((others, steps)), dma((others, steps)), dma((steps,)), dma((steps,)),
             dma((depth,)), dma((depth,)), dma((depth,)), dma((depth,)),
@@ -367,7 +411,10 @@
         compiler_params=pltpu.CompilerParams(
             collective_id=0, has_side_effects=True, vmem_limit_bytes=60 * 1024 * 1024
         ),
-    )(activations, gradients, act_history, grad_history, owner_rank[None, :])
+    )(
+        activations, gradients.T, act_history, grad_history,
+        owner_rank[None, :], act_slots[None, :], grad_slots[None, :],
+    )
 
 
 def gathered_sums(activations, gradients, act_history, grad_history, owner_rank):
@@ -395,8 +442,16 @@
     column_total = gradients.shape[1]
     row_count = model_width // dp
     fits = dp % (CORES * ROWS_Y) == 0 and (row_count * CORES) % LANES == 0
-    sums = fused_sums if fits else gathered_sums
-    summed, current, act_peak, grad_peak = sums(
+    fits = fits and column_total % SUBLANES == 0
+    act_slots = history_slot[:model_width]
+    grad_slots = lax.dynamic_slice_in_dim(
+        history_slot, model_width + lax.axis_index("tensor") * column_total, column_total, 0
+    )
+    if fits:
+        return fused_outputs(
+            activations, gradients, act_history, grad_history, owner_rank, act_slots, grad_slots
+        )
+    summed, current, act_peak, grad_peak = gathered_sums(
         activations, gradients, act_history, grad_history, owner_rank
     )
     act_scale = QUANT_LIMIT / jnp.maximum(jnp.max(current, axis=0), SCALE_FLOOR)
@@ -405,10 +460,6 @@
     row_base = lax.axis_index("dp") * row_count
     row_scale = lax.dynamic_slice_in_dim(act_scale, row_base, row_count, 0)
     weight_grad = summed / (row_scale[:, None] * grad_scale[None, :]) * grad_factor
-    act_slots = history_slot[:model_width]
-    grad_slots = lax.dynamic_slice_in_dim(
-        history_slot, model_width + lax.axis_index("tensor") * column_total, column_total, 0
-    )
     act_history_out = place_peaks(current, act_peak[0], act_slots)[None]
     grad_history_out = place_peaks(grad_history, grad_peak[0], grad_slots)
     return (weight_grad, act_history_out, grad_history_out)

time: 93.4 us -> 84.7 us (0.907)
  local copies, waits for them, and re-layouts: 15.6 us -> 7.77 us
  other arithmetic: 5.08 us -> 0 us
  Pallas kernels: 71.4 us -> 75.9 us
    unnamed x5 -> x3, local copies, waits for them, and re-layouts: 15.5 us -> 5.09 us
    pallas_call x1, Pallas kernels: 71.4 us -> 75.9 us  [fused_outputs(): pl.pallas_call(functools.partial(fused_kernel, dp, tensor), out_shape=(ja...]
    mul x1 -> x0, other arithmetic: 2.15 us -> none  [body(): summed / (row_scale[:, None] * grad_scale[None, :]) * grad_factor]
    broadcast_in_dim x1 -> x0, other arithmetic: 1.48 us -> none  [body(): act_history_out = place_peaks(current, act_peak[0], act_slots)[None]]
    slice x2 -> x1, local copies, waits for them, and re-layouts: 0.01 us -> 1.28 us  [body(): act_slots = history_slot[:model_width]]
where the time goes in v2:
time: 84.7 us; the launch traced here: 84.4 us
  Pallas kernels  75.9 us (90%)
  local copies, waits for them, and re-layouts  7.77 us (9%)
    pallas_call x1, Pallas kernels, fused_outputs(): pl.pallas_call(functools.partial(fused_kernel, dp, tensor), out_shape=(ja...  75.9 us
    unnamed x3, local copies, waits for them, and re-layouts  5.09 us

profile of v2, /device:TPU:0, one launch (start us, length us, event | category | flops | bytes accessed | tf_op | source)
XLA Modules:
  0.0 84.4 jit_solution(14750808910892024585)
XLA Ops:
  0.6 1.3 %slice.3 = s32[1024]{0:T(1024)} slice(s32[6496]{0:T(1024)} %param.11), slice={[0:1024]} | slice | bytes 8192 | tf_op jit(solution)/shard_map/slice | solution.py:446
  1.9 0.8 dynamic_slice.3
  2.7 0.6 broadcast_in_dim.11.grad_slot_ref
  3.3 75.9 %shard_map.85 = (f32[64,2736]{1,0:T(8,128)}, f32[1,16,1024]{2,1,0:T(8,128)}, f32[16,2736]{1,0:T(8,128)}) custom-call(bf16[1024,1024]{1,0:T(8,128)(2,1)} %act_hbm.1, bf16[2736,2048]{1,0:T(8,128)(2,1)} %bitcast.3, f32[1,16,1024]{2,1,0:T(8,128)} %act_hist_ref.1, f32[16,2736]{1,0:T(8,128)} %grad_hist_ref.1, s32[1,1024]{1,0:T(1,128)} %bitcast.5, ...), custom_call_target="tpu_custom_call" | custom-call | tf_op jit(solution)/shard_map/pallas_call | solution.py:377
  79.3 2.0 %copy.12 = f32[64,2736]{1,0:T(8,128)} copy(f32[64,2736]{1,0:T(8,128)} %get-tuple-element.6) | data formatting | bytes 1400832
  81.3 1.5 %copy.13 = f32[1,16,1024]{2,1,0:T(8,128)} copy(f32[1,16,1024]{2,1,0:T(8,128)} %get-tuple-element.7) | data formatting | bytes 131072
  82.8 1.6 %copy.14 = f32[16,2736]{1,0:T(8,128)} copy(f32[16,2736]{1,0:T(8,128)} %get-tuple-element.8) | data formatting | bytes 350208

commit v3 on v2

--- a/solution.py
+++ b/solution.py
@@ -14,7 +14,7 @@
 ROWS_Y = 2
 LANES = 128
 SUBLANES = 16
-COL_TILE = 512
+COL_TILE = 1408
 MESH = pl.DeviceIdType.MESH
 
 
@@ -34,7 +34,7 @@
 
 def fused_kernel(
     dp, tensor,
-    act_hbm, grad_hbm, act_hist_ref, grad_hist_ref, owner_ref, act_slot_ref, grad_slot_ref,
+    act_hbm, grad_hbm, act_hist_ref, grad_hist_ref, owner_ref, slot_ref,
     weight_ref, act_hist_out, grad_hist_out,
     act_own, act_got, hist_got, gq, part, core_got, y_out, y_got, z_out, z_got,
     lhs, peaks, act_peaks, act_scale, grad_scale, scale_down, peak_down, row_undo, current_hist,
@@ -95,6 +95,9 @@
         y = yy * k + (1 - yy) * (1 - k)
         return pl.ds(pl.multiple_of((target_z(u) * ROWS_Y + y) * pair, LANES), pair)
 
+    def line_cols(u):
+        return pl.ds(pl.multiple_of(target_z(u) * (ROWS_Y * pair), LANES), ROWS_Y * pair)
+
     def hist_copy(t):
         return pltpu.make_async_remote_copy(
             src_ref=act_hist_ref.at[0], dst_ref=hist_got.at[t - 1],
@@ -110,10 +113,16 @@
             device_id={"tensor": lax.rem(mt + t, tensor)}, device_id_type=MESH,
         )
 
-    def core_copy(s):
-        return pltpu.make_async_remote_copy(
-            src_ref=part.at[s, pl.ds(pl.multiple_of((1 - core) * block, block), block)],
-            dst_ref=core_got.at[s],
+    def side(k):
+        return yy * k + (1 - yy) * (1 - k)
+
+    def half_rows(k, c):
+        return pl.ds(pl.multiple_of(side(k) * pair + c * block, block), block)
+
+    def core_copy(u, k):
+        s = u * 2 + k
+        return pltpu.make_async_remote_copy(
+            src_ref=part.at[u, half_rows(k, 1 - core)], dst_ref=core_got.at[s],
             send_sem=core_send.at[s], recv_sem=core_recv.at[s],
             device_id={"dp": sibling}, device_id_type=MESH,
         )
@@ -234,24 +243,18 @@
     )
 
     def load_lhs(read, at):
-        scaled = read.astype(jnp.float32) * act_scale[:, at]
-        scaled = jnp.clip(scaled, -QUANT_LIMIT, QUANT_LIMIT)
-        lhs[...] = jnp.transpose(scaled).astype(jnp.bfloat16)
-
-    def multiply(s, source, first):
+        return jnp.transpose(quantize(read, act_scale[:, at]))
+
+    def multiply(put, left, source):
         at = pl.ds(pl.multiple_of(source * tokens, tokens), tokens)
         full = cols // COL_TILE
 
         def one(start, size):
             here = pl.ds(start, size)
-            term = lax.dot_general(
-                lhs[...], gq[here, at], (((1,), (1,)), ((), ())),
+            put(here, lax.dot_general(
+                left[...], gq[here, at], (((1,), (1,)), ((), ())),
                 preferred_element_type=jnp.float32,
-            )
-            if first:
-                part[s, :, here] = term
-            else:
-                part[s, :, here] += term
+            ))
 
         def tile(j, carry):
             one(pl.multiple_of(j * COL_TILE, COL_TILE), COL_TILE)
@@ -261,24 +264,31 @@
         if cols % COL_TILE:
             one(full * COL_TILE, cols % COL_TILE)
 
-    mine = pl.ds(pl.multiple_of(core * block, block), block)
-
-    def own_product(u, k):
-        at = block_cols(u, k)
-        load_lhs(act_own[:, at], at)
-        multiply(u * 2 + k, mt, True)
+    def own_product(u):
+        at = line_cols(u)
+        lhs[...] = load_lhs(act_own[:, at], at)
+
+        def put(here, term):
+            part[u, :, here] = term
+
+        multiply(put, lhs, mt)
 
     def got_product(u, k):
         at = block_cols(u, k)
+        down = pl.ds(pl.multiple_of(side(k) * pair, pair), pair)
+
+        def put(here, term):
+            part[u, down, here] += term
+
         for t in range(1, tensor):
             x_copy(t, u, k).wait_recv()
-            load_lhs(act_got[t - 1, :, at], at)
-            multiply(u * 2 + k, lax.rem(mt + tensor - t, tensor), False)
-        core_copy(u * 2 + k).start()
+            lhs[:pair, :] = load_lhs(act_got[t - 1, :, at], at)
+            multiply(put, lhs.at[:pair], lax.rem(mt + tensor - t, tensor))
+        core_copy(u, k).start()
 
     def core_sum(u, k):
-        core_copy(u * 2 + k).wait_recv()
-        return part[u * 2 + k, mine, :] + core_got[u * 2 + k]
+        core_copy(u, k).wait_recv()
+        return part[u, half_rows(k, core), :] + core_got[u * 2 + k]
 
     def send_y(u):
         y_out[u] = core_sum(u, 0).astype(jnp.bfloat16)
@@ -288,18 +298,21 @@
         y_copy(u).wait_recv()
         return core_sum(u, 1) + y_got[u].astype(jnp.float32)
 
-    own_product(0, 0)
+    own_product(0)
     got_product(0, 0)
-    own_product(*((1, 0) if depth > 1 else (0, 1)))
+    if depth > 1:
+        own_product(1)
     send_y(0)
 
     def unit(u, carry):
         got_product(u + 1, 0)
-        own_product(u, 1)
+
+        @pl.when(u + 2 < depth)
+        def _():
+            own_product(u + 2)
+
         send_y(u + 1)
         got_product(u, 1)
-        last = lax.div(u + 2, depth)
-        own_product(u + 2 - last, last)
         z_out[u] = line_sum(u).astype(jnp.bfloat16)
         z_copy(u).start()
         return carry
@@ -316,8 +329,12 @@
     for t in range(1, tensor):
         act_peak_copy(t).start()
     hist_row = lax.broadcasted_iota(jnp.int32, grad_hist_ref.shape, 0)
+    grad_slots = slot_ref[:, width:width + cols]
+    for t in range(1, tensor):
+        first = width + t * cols
+        grad_slots = jnp.where(mt == t, slot_ref[:, first:first + cols], grad_slots)
     grad_hist_out[...] = jnp.where(
-        hist_row == grad_slot_ref[...], tops[:, width:width + cols], grad_hist_ref[...]
+        hist_row == grad_slots, tops[:, width:width + cols], grad_hist_ref[...]
     )
 
     picks = lax.broadcasted_iota(jnp.int32, (block, width), 1) == (
@@ -332,7 +349,7 @@
         act_peak_copy(t).wait()
     hist_row = lax.broadcasted_iota(jnp.int32, current_hist.shape, 0)
     act_hist_out[0] = jnp.where(
-        hist_row == act_slot_ref[...], jnp.max(act_peaks[...], axis=0), current_hist[...]
+        hist_row == slot_ref[:, :width], jnp.max(act_peaks[...], axis=0), current_hist[...]
     )
 
     got_product(depth - 1, 1)
@@ -346,7 +363,7 @@
         for k in range(2):
             for t in range(1, tensor):
                 x_copy(t, u, k).wait_send()
-            core_copy(u * 2 + k).wait_send()
+            core_copy(u, k).wait_send()
         y_copy(u).wait_send()
         return carry
 
@@ -359,7 +376,7 @@
     lax.fori_loop(0, depth - 1, finish_z, 0)
 
 
-def fused_outputs(activations, gradients, act_history, grad_history, owner_rank, act_slots, grad_slots):
+def fused_outputs(activations, gradients, act_history, grad_history, owner_rank, history_slot):
     dp, tensor = lax.axis_size("dp"), lax.axis_size("tensor")
     tokens, width = activations.shape
     rows, cols = gradients.shape
@@ -381,20 +398,20 @@
             jax.ShapeDtypeStruct((1, hist, width), f32),
             jax.ShapeDtypeStruct((hist, cols), f32),
         ),
-        in_specs=[hbm, hbm, vmem, vmem, vmem, vmem, vmem],
+        in_specs=[hbm, hbm, vmem, vmem, vmem, vmem],
         out_specs=(vmem, vmem, vmem),
         scratch_shapes=[
             pltpu.VMEM((tokens, width), bf16),
             pltpu.VMEM((others, tokens, width), bf16),
             pltpu.VMEM((others, hist, width), f32),
             pltpu.VMEM((cols, rows), bf16),
-            pltpu.VMEM((steps, block * CORES, cols), f32),
+            pltpu.VMEM((depth, ROWS_Y * CORES * block, cols), f32),
             pltpu.VMEM((steps, block, cols), f32),
             pltpu.VMEM((depth, block, cols), bf16),
             pltpu.VMEM((depth, block, cols), bf16),
             pltpu.VMEM((depth, block, cols), bf16),
             pltpu.VMEM((depth, block, cols), bf16),
-            pltpu.VMEM((block * CORES, tokens), bf16),
+            pltpu.VMEM((ROWS_Y * CORES * block, tokens), bf16),
             pltpu.VMEM((dp, 1, width + padded), f32),
             pltpu.VMEM((tensor, 1, width), f32),
             pltpu.VMEM((1, width), f32),
@@ -413,8 +430,25 @@
         ),
     )(
         activations, gradients.T, act_history, grad_history,
-        owner_rank[None, :], act_slots[None, :], grad_slots[None, :],
-    )
+        owner_rank[None, :], history_slot[None, :],
+    )
+
+
+def hand_over_kernel(*refs):
+    half = len(refs) // 2
+    for source, target in zip(refs[:half], refs[half:]):
+        target[...] = source[...]
+
+
+def hand_over(*results):
+    vmem = pl.BlockSpec(memory_space=pltpu.VMEM)
+    return pl.pallas_call(
+        hand_over_kernel,
+        out_shape=tuple(jax.ShapeDtypeStruct(r.shape, r.dtype) for r in results),
+        in_specs=[vmem] * len(results),
+        out_specs=(vmem,) * len(results),
+        compiler_params=pltpu.CompilerParams(vmem_limit_bytes=4 * 1024 * 1024),
+    )(*results)
 
 
 def gathered_sums(activations, gradients, act_history, grad_history, owner_rank):
@@ -443,14 +477,14 @@
     row_count = model_width // dp
     fits = dp % (CORES * ROWS_Y) == 0 and (row_count * CORES) % LANES == 0
     fits = fits and column_total % SUBLANES == 0
+    if fits:
+        return hand_over(*fused_outputs(
+            activations, gradients, act_history, grad_history, owner_rank, history_slot
+        ))
     act_slots = history_slot[:model_width]
     grad_slots = lax.dynamic_slice_in_dim(
         history_slot, model_width + lax.axis_index("tensor") * column_total, column_total, 0
     )
-    if fits:
-        return fused_outputs(
-            activations, gradients, act_history, grad_history, owner_rank, act_slots, grad_slots
-        )
     summed, current, act_peak, grad_peak = gathered_sums(
         activations, gradients, act_history, grad_history, owner_rank
     )

time: 84.7 us -> 75.7 us (0.89)
  Pallas kernels: 75.9 us -> 70.5 us
  local copies, waits for them, and re-layouts: 7.77 us -> 4.24 us
    pallas_call x1, Pallas kernels: 75.9 us -> 69.5 us  [fused_outputs(): pl.pallas_call(functools.partial(fused_kernel, dp, tensor), out_shape=(ja...]
    unnamed x3 -> x6, local copies, waits for them, and re-layouts: 5.09 us -> 2.86 us
    slice x1 -> x0, local copies, waits for them, and re-layouts: 1.28 us -> none  [body(): act_slots = history_slot[:model_width]]
    pallas_call x0 -> x1, Pallas kernels: none -> 0.99 us  [hand_over(): pl.pallas_call(hand_over_kernel, out_shape=tuple((jax.ShapeDtypeStruct(r....]
where the time goes in v3:
time: 75.7 us; the launch traced here: 75.4 us
  Pallas kernels  70.5 us (93%)
  local copies, waits for them, and re-layouts  4.24 us (6%)
    pallas_call x1, Pallas kernels, fused_outputs(): pl.pallas_call(functools.partial(fused_kernel, dp, tensor), out_shape=(ja...  69.5 us
    unnamed x6, local copies, waits for them, and re-layouts  2.86 us

profile of v3, /device:TPU:0, one launch (start us, length us, event | category | flops | bytes accessed | tf_op | source)
XLA Modules:
  0.0 75.4 jit_solution(1421992673802967529)
XLA Ops:
  0.6 1.4 %broadcast_in_dim.7.slot_ref = s32[1,6496]{1,0:T(1,128)} reshape(s32[6496]{0:T(1024)} %param.11) | data formatting | bytes 51968 | tf_op jit(solution)/shard_map/broadcast_in_dim | solution.py:433
  2.0 69.5 %shard_map.85 = (f32[64,2736]{1,0:T(8,128)}, f32[1,16,1024]{2,1,0:T(8,128)}, f32[16,2736]{1,0:T(8,128)}) custom-call(bf16[1024,1024]{1,0:T(8,128)(2,1)} %act_hbm.1, bf16[2736,2048]{1,0:T(8,128)(2,1)} %bitcast.2, f32[1,16,1024]{2,1,0:T(8,128)} %act_hist_ref.1, f32[16,2736]{1,0:T(8,128)} %grad_hist_ref.1, s32[1,1024]{1,0:T(1,128)} %bitcast.3, ...), custom_call_target="tpu_custom_call" | custom-call | tf_op jit(solution)/shard_map/pallas_call | solution.py:394
  71.5 0.0 copy-start
  71.5 1.1 %copy-done = f32[64,2736]{1,0:T(8,128)S(1)} copy-done((f32[64,2736]{1,0:T(8,128)S(1)}, f32[64,2736]{1,0:T(8,128)}, u32[]{:S(2)}) %copy-start) | copy-done | bytes 700440
  72.6 0.0 copy-start.1
  72.6 0.9 %copy-done.1 = f32[16,2736]{1,0:T(8,128)S(1)} copy-done((f32[16,2736]{1,0:T(8,128)S(1)}, f32[16,2736]{1,0:T(8,128)}, u32[]{:S(2)}) %copy-start.1) | copy-done | bytes 175128
  73.6 0.0 copy-start.2
  73.6 0.8 %copy-done.2 = f32[1,16,1024]{2,1,0:T(8,128)S(1)} copy-done((f32[1,16,1024]{2,1,0:T(8,128)S(1)}, f32[1,16,1024]{2,1,0:T(8,128)}, u32[]{:S(2)}) %copy-start.2) | copy-done | bytes 65560
  74.4 1.0 %shard_map.86 = (f32[64,2736]{1,0:T(8,128)}, f32[1,16,1024]{2,1,0:T(8,128)}, f32[16,2736]{1,0:T(8,128)}) custom-call(f32[64,2736]{1,0:T(8,128)S(1)} %copy-done, f32[1,16,1024]{2,1,0:T(8,128)S(1)} %copy-done.2, f32[16,2736]{1,0:T(8,128)S(1)} %copy-done.1), custom_call_target="tpu_custom_call" | custom-call | tf_op jit(solution)/shard_map/pallas_call | solution.py:445
Async XLA Ops:
  71.5 1.1 %copy-start = (f32[64,2736]{1,0:T(8,128)S(1)}, f32[64,2736]{1,0:T(8,128)}, u32[]{:S(2)}) copy-start(f32[64,2736]{1,0:T(8,128)} %get-tuple-element.6.refs_0_) | copy-start | bytes 2101252
  72.6 0.9 %copy-start.1 = (f32[16,2736]{1,0:T(8,128)S(1)}, f32[16,2736]{1,0:T(8,128)}, u32[]{:S(2)}) copy-start(f32[16,2736]{1,0:T(8,128)} %get-tuple-element.8.refs_2_) | copy-start | bytes 525316
  73.6 0.8 %copy-start.2 = (f32[1,16,1024]{2,1,0:T(8,128)S(1)}, f32[1,16,1024]{2,1,0:T(8,128)}, u32[]{:S(2)}) copy-start(f32[1,16,1024]{2,1,0:T(8,128)} %get-tuple-element.7.refs_1_) | copy-start | bytes 196612
